TPU v7x, 32 devices: a whole 2x2x4 slice. The times are simulated.
32 devices in a mesh: group: 2 (over y), expert: 4 (over z), tensor: 2 (over x), sub: 2 (over core).
Axes of the slice: x: 2, y: 2, z: 4, core: 2. Of those that a mesh axis runs over, the one named last changes fastest.
Arguments:
- tokens: bfloat16 [64, 7168], P(('group', 'expert', 'sub')), parts along dimension 0, may hold values from -6 to 6
- expert_ids: int32 [64, 2], P(('group', 'expert', 'sub')), parts along dimension 0, may hold values from 0 to 1, all different within a row; in each aligned block of 4 rows (0 to 3, 4 to 7, ...) at most 4 rows name the same one
- gate_codes: int32 [64, 2], P(('group', 'expert', 'sub')), parts along dimension 0, may hold values from 1 to 63
- w_gate: bfloat16 [4, 1024, 7168], P('expert', ('tensor', 'sub')), may hold values from -0.0625 to 0.0625
- w_up: bfloat16 [4, 1024, 7168], P('expert', ('tensor', 'sub')), may hold values from -0.0625 to 0.0625
- w_down: bfloat16 [4, 1024, 7168], P('expert', ('tensor', 'sub')), may hold values from -0.125 to 0.125
Outputs:
- mixed: bfloat16 [64, 7168], P(('group', 'expert', 'sub'), 'tensor'), parts along dimension 0
There are 2 independent parts, one for each index of `group`. A program takes and returns all parts, laid end to end along the dimension named above; an argument that names none is the same for every part. Nothing has to cross between parts.
Inputs may be any that keep to these rules, and one draw needn't show every extreme that they name: `expert_ids`: the 2 numbers of a row differ; within the rows of one device (aligned blocks of 4 rows) no expert is named by more than 4 rows, a bound that some block reaches.
All inputs are finite; a program needn't handle non-finite values.
Results may differ from a plain program's by a relative error of at most 0.008.
Values may be sent and summed in bfloat16 or wider, within the bound.
A program may use at most 64 MiB of HBM per device.

v0:
```python
import jax
import jax.numpy as jnp
from jax import lax
from jax.sharding import PartitionSpec as P


def shards(tokens, expert_ids, gate_codes, w_gate, w_up, w_down):
    tok_rows, features = tokens.shape
    per_token = expert_ids.shape[1]
    owners = lax.axis_size("expert")
    sub_count = lax.axis_size("sub")
    tensor_count = lax.axis_size("tensor")
    experts = owners // 2
    capacity = min(tok_rows, tok_rows * per_token // experts + 1)
    flat_ids = expert_ids.reshape(-1)
    matches = (flat_ids[:, None] == jnp.arange(experts, dtype=jnp.int32)[None, :]).astype(jnp.int32)
    before = jnp.cumsum(matches, axis=0) - matches
    slot_index = jnp.sum(before * matches, axis=1)
    position = flat_ids * capacity + slot_index
    onehot = position[:, None] == jnp.arange(experts * capacity, dtype=jnp.int32)[None, :]
    weights = gate_codes.reshape(-1).astype(jnp.float32) / 64.0
    choose = jnp.any(onehot.reshape(tok_rows, per_token, -1), axis=1).astype(jnp.bfloat16)
    combine = jnp.sum(
        jnp.where(onehot, weights[:, None], 0.0).reshape(tok_rows, per_token, -1), axis=1
    )
    packed = jnp.dot(choose.T, tokens, preferred_element_type=jnp.float32).astype(jnp.bfloat16)
    outgoing = jnp.broadcast_to(
        packed.reshape(experts, 1, capacity, features), (experts, 2, capacity, features)
    )
    arrived = lax.all_to_all(
        outgoing.reshape(owners, capacity, features),
        "expert",
        split_axis=0,
        concat_axis=0,
        tiled=True,
    )
    slot_rows = lax.all_gather(arrived, "sub", axis=1, tiled=True).reshape(-1, features)
    contract = (((1,), (1,)), ((), ()))
    gate_act = lax.dot_general(slot_rows, w_gate[0], contract, preferred_element_type=jnp.float32)
    up_act = lax.dot_general(slot_rows, w_up[0], contract, preferred_element_type=jnp.float32)
    hidden = (jax.nn.silu(gate_act) * up_act).astype(jnp.bfloat16)
    partial_value = jnp.dot(hidden, w_down[0], preferred_element_type=jnp.float32).astype(
        jnp.bfloat16
    )
    partial_value = partial_value.reshape(owners, sub_count, capacity, features)
    block = features // tensor_count
    sectioned = partial_value.reshape(owners, sub_count, capacity, tensor_count, block).transpose(
        0, 2, 3, 1, 4
    )
    sectioned = sectioned.reshape(owners, capacity, tensor_count * sub_count, block)
    gathered = lax.all_to_all(sectioned, ("tensor", "sub"), split_axis=2, concat_axis=2, tiled=True)
    run_total = jnp.sum(gathered.astype(jnp.float32), axis=2)
    came_back = lax.all_to_all(run_total, "expert", split_axis=0, concat_axis=0, tiled=True)
    summed = jnp.sum(came_back.reshape(experts, 2, capacity, block), axis=1)
    mixed = jnp.dot(
        combine,
        summed.reshape(-1, block),
        precision=lax.Precision.HIGHEST,
        preferred_element_type=jnp.float32,
    )
    return mixed.astype(jnp.bfloat16)


def solution(mesh):
    return jax.shard_map(
        shards,
        mesh=mesh,
        in_specs=(
            P(("group", "expert", "sub"), None),
            P(("group", "expert", "sub"), None),
            P(("group", "expert", "sub"), None),
            P("expert", ("tensor", "sub"), None),
            P("expert", ("tensor", "sub"), None),
            P("expert", ("tensor", "sub"), None),
        ),
        out_specs=P(("group", "expert", "sub"), "tensor"),
        check_vma=False,
    )
```

profile of v0, /device:TPU:0, one launch (start us, length us, event | category | flops | bytes accessed | tf_op | source)
XLA Modules:
  0.0 52.1 jit_solution(3260446464871624267)
XLA Ops:
  0.0 0.0 copy-start
  0.0 0.8 %copy.34 = s32[4,2]{1,0:T(4,128)S(1)} copy(s32[4,2]{0,1:T(2,128)} %param.7) | data formatting | bytes 64 | tf_op args[1]
  0.8 0.1 eq.30
  0.9 0.2 reduce_window_sum.11
  1.1 0.1 reduce_sum.39
  1.2 0.1 copy.36
  1.3 0.1 fusion.25
  1.4 0.0 copy-done
  1.4 0.2 convolution_convert_fusion.1
  1.6 0.1 broadcast_in_dim.25
  1.6 0.1 broadcast_in_dim.26
  1.7 14.3 %all_to_all.15 = bf16[4,4,7168]{2,1,0:T(4,128)(2,1)S(1)} all-to-all(bf16[4,4,7168]{2,1,0:T(4,128)(2,1)S(1)} %bitcast.32), channel_id=1, replica_groups=mesh['group'=2,'expert'=4,'tensor'=2,'sub'=2] {'expert'}, dimensions={0} | all-to-all | bytes 458752 | tf_op jit(solution)/shard_map/all_to_all | solution.py:30
  16.0 0.1 copy.37
  16.2 2.1 %all_gather.3 = bf16[4,8,7168]{2,0,1:T(4,128)(2,1)S(1)} all-gather(bf16[4,4,7168]{2,0,1:T(4,128)(2,1)S(1)} %copy.37), channel_id=1, replica_groups=mesh['group'=2,'expert'=4,'tensor'=2,'sub'=2] {'sub'}, dimensions={1}, use_global_device_ids=true | all-gather | bytes 688128 | tf_op jit(solution)/shard_map/all_gather | solution.py:37
  18.3 3.2 %fusion.3 = f32[32,256]{1,0:T(8,128)S(1)} fusion(bf16[1,256,7168]{2,1,0:T(8,128)(2,1)} %param.9, bf16[4,8,7168]{2,0,1:T(4,128)(2,1)S(1)} %all_gather.3), kind=kOutput, calls=%fused_computation.6 | convolution fusion | flops 117440512 | bytes 4161536 | tf_op jit(solution)/shard_map/dot_general | solution.py:39
  21.5 5.7 %convolution_convert_fusion = bf16[32,7168]{1,0:T(8,128)(2,1)S(1)} fusion(bf16[1,256,7168]{2,1,0:T(8,128)(2,1)} %param.11, bf16[1,256,7168]{2,1,0:T(8,128)(2,1)} %param.10, bf16[4,8,7168]{2,0,1:T(4,128)(2,1)S(1)} %all_gather.3, f32[32,256]{1,0:T(8,128)S(1)} %fusion.3), kind=kOutput, calls=%fused_computation | convolution fusion | flops 235159552 | bytes 8290304 | tf_op jit(solution)/shard_map/dot_general | solution.py:42
  27.3 0.0 copy-start.1
  27.3 0.3 reshape_reshape.3
  27.6 0.2 copy.41
  27.8 10.7 %all_to_all.16 = bf16[4,4,4,3584]{3,1,0,2:T(4,128)(2,1)S(1)} all-to-all(bf16[4,4,4,3584]{3,1,0,2:T(4,128)(2,1)S(1)} %bitcast.31), channel_id=1, replica_groups=mesh['group'=2,'expert'=4,'tensor'=2,'sub'=2] {'tensor','sub'}, dimensions={2} | all-to-all | bytes 917504 | tf_op jit(solution)/shard_map/all_to_all | solution.py:51
  38.5 0.9 %convert_reduce_fusion = f32[4,4,3584]{2,1,0:T(4,128)} fusion(bf16[4,4,4,3584]{3,1,0,2:T(4,128)(2,1)S(1)} %all_to_all.16), kind=kLoop, calls=%fused_computation.10 | loop fusion | flops 401408 | bytes 688128 | tf_op jit(solution)/shard_map/reduce_sum | solution.py:52
  39.4 3.4 %all-to-all-start.2 = ((f32[4,4,3584]{2,1,0:T(4,128)}), f32[4,4,3584]{2,1,0:T(4,128)S(1)}, u32[]{:S(2)}, u32[]{:S(2)}) async-start(f32[4,4,3584]{2,1,0:T(4,128)} %convert_reduce_fusion), calls=%async_computation.2 | async-start | bytes 458752 | tf_op jit(solution)/shard_map/all_to_all | solution.py:53
  42.8 0.0 copy-done.1
  42.8 0.1 select_reduce_fusion
  42.9 8.3 %all-to-all-done.2 = f32[4,4,3584]{2,1,0:T(4,128)S(1)} async-done(((f32[4,4,3584]{2,1,0:T(4,128)}), f32[4,4,3584]{2,1,0:T(4,128)S(1)}, u32[]{:S(2)}, u32[]{:S(2)}) %all-to-all-start.2) | async-done | bytes 229408 | tf_op jit(solution)/shard_map/all_to_all | solution.py:53
  51.2 0.9 %convolution_convert_fusion.2 = bf16[4,3584]{1,0:T(4,128)(2,1)} fusion(f32[4,8]{1,0:T(4,128)S(1)} %select_reduce_fusion, f32[8,3584]{1,0:T(8,128)S(1)} %reshape.60), kind=kOutput, calls=%fused_computation.2 | convolution fusion | flops 1390592 | bytes 143488 | tf_op jit(solution)/shard_map/dot_general | solution.py:55
  (6 shorter events, 0.1 us)
Async XLA Ops:
  0.0 1.4 %copy-start = (bf16[4,7168]{1,0:T(4,128)(2,1)S(1)}, bf16[4,7168]{1,0:T(4,128)(2,1)}, u32[]{:S(2)}) copy-start(bf16[4,7168]{1,0:T(4,128)(2,1)} %param.6) | copy-start | bytes 172036
  27.3 15.5 %copy-start.1 = (s32[4,2]{0,1:T(2,128)S(1)}, s32[4,2]{0,1:T(2,128)}, u32[]{:S(2)}) copy-start(s32[4,2]{0,1:T(2,128)} %param.8) | copy-start | bytes 100
  39.4 11.8 %all-to-all-start.2 = ((f32[4,4,3584]{2,1,0:T(4,128)}), f32[4,4,3584]{2,1,0:T(4,128)S(1)}, u32[]{:S(2)}, u32[]{:S(2)}) async-start(f32[4,4,3584]{2,1,0:T(4,128)} %convert_reduce_fusion), calls=%async_computation.2 | async-start | bytes 458752 | tf_op jit(solution)/shard_map/all_to_all | solution.py:53
where the time goes:
time: 52.5 us; the launch traced here: 52.1 us
  blocking collectives  27.1 us (52%)
  matrix products  10 us (19%)
  waiting for transfers between devices  8.28 us (16%)
  starting transfers between devices  3.38 us (6%)
  local copies, waits for them, and re-layouts  1.83 us (3%)
  other arithmetic  1.33 us (3%)
    all_to_all x1, blocking collectives, shards(): lax.all_to_all(outgoing.reshape(owners, capacity, features), 'expert', sp...  14.3 us
    all_to_all x1, blocking collectives, shards(): lax.all_to_all(sectioned, ('tensor', 'sub'), split_axis=2, concat_axis=2,...  10.7 us
    all_to_all x1, waiting for transfers between devices, shards(): lax.all_to_all(run_total, 'expert', split_axis=0, concat_axis=0, tiled=True)  8.28 us
    dot_general x1, matrix products, shards(): jnp.dot(hidden, w_down[0], preferred_element_type=jnp.float32)  5.73 us
    all_to_all x1, starting transfers between devices, shards(): lax.all_to_all(run_total, 'expert', split_axis=0, concat_axis=0, tiled=True)  3.38 us
    dot_general x1, matrix products, shards(): lax.dot_general(slot_rows, w_gate[0], contract, preferred_element_type=jn...  3.23 us
    all_gather x1, blocking collectives, shards(): lax.all_gather(arrived, 'sub', axis=1, tiled=True).reshape(-1, features)  2.13 us
  transfers between devices with their start and end apart: 1, of which 1 were waited for; matrix products, arithmetic and copies ran while one was open for 0% of the time, Pallas kernels for 0%

commit v1 on v0

v1 whole, which is shorter than its diff:
```python
import functools

import jax
import jax.numpy as jnp
from jax import lax
from jax.experimental import pallas as pl
from jax.experimental.pallas import tpu as pltpu
from jax.sharding import PartitionSpec as P

MESH = pl.DeviceIdType.MESH


def split_count(width, most):
    parts = most
    while width % (parts * 128):
        parts -= 1
    return parts


def layer(
    E, X, K, C,
    tok_hbm, ids_hbm, codes_hbm, wg_hbm, wu_hbm, wd_hbm,
    out_ref,
    gat, xs, ids_v, codes_v, wg, wu, wd,
    keep, d_out, d_in, b_out, b_in, c_out, c_in,
    small_sem, wg_sem, wu_sem, wd_sem,
    z_send, z_recv, f_send, f_recv, d_send, d_recv, b_send, b_recv, c_send, c_recv,
):
    T, D = tok_hbm.shape
    half = E * T
    kw = D // K
    block = D // X
    cw = block // C
    e = lax.axis_index("expert")
    x = lax.axis_index("tensor")
    s = lax.axis_index("sub")
    partner = {"sub": 1 - s}

    tok_copy = pltpu.make_async_copy(tok_hbm, gat.at[0, e], small_sem.at[0])
    tok_copy.start()
    ids_copy = pltpu.make_async_copy(ids_hbm, ids_v, small_sem.at[1])
    codes_copy = pltpu.make_async_copy(codes_hbm, codes_v, small_sem.at[2])
    ids_copy.start()
    codes_copy.start()

    barrier = pltpu.get_barrier_semaphore()
    for d in range(1, E):
        pl.semaphore_signal(barrier, inc=1, device_id={"expert": (e + d) % E}, device_id_type=MESH)
    for d in range(1, X):
        pl.semaphore_signal(barrier, inc=1, device_id={"tensor": (x + d) % X}, device_id_type=MESH)
    pl.semaphore_signal(barrier, inc=1, device_id=partner, device_id_type=MESH)

    g_copies, u_copies, w_copies = [], [], {}
    for k in range(K):
        cols = pl.ds(k * kw, kw)
        g_copies.append(pltpu.make_async_copy(wg_hbm.at[0, :, cols], wg.at[k], wg_sem.at[k]))
        u_copies.append(pltpu.make_async_copy(wu_hbm.at[0, :, cols], wu.at[k], wu_sem.at[k]))
        g_copies[k].start()
        u_copies[k].start()
    order = [(i, c) for i in list(range(1, X)) + [0] for c in range(C)]
    for i, c in order:
        first = pl.multiple_of(((x + i) % X) * block + c * cw, 128)
        w_copies[i, c] = pltpu.make_async_copy(
            wd_hbm.at[0, :, pl.ds(first, cw)], wd.at[i, c], wd_sem.at[i, c]
        )
        w_copies[i, c].start()

    tok_copy.wait()
    pl.semaphore_wait(barrier, E - 1 + X - 1 + 1)

    def z_copy(d, k, slot):
        piece = gat.at[0, slot, :, pl.ds(k * kw, kw)]
        return pltpu.make_async_remote_copy(
            src_ref=piece, dst_ref=piece, send_sem=z_send.at[d, k], recv_sem=z_recv.at[d, k],
            device_id={"expert": (e + d) % E}, device_id_type=MESH,
        )

    def f_copy(d, k):
        slot = (e + E - d) % E
        cols = pl.ds(k * kw, kw)
        return pltpu.make_async_remote_copy(
            src_ref=gat.at[0, slot, :, cols], dst_ref=gat.at[1, slot, :, cols],
            send_sem=f_send.at[d, k], recv_sem=f_recv.at[d, k],
            device_id=partner, device_id_type=MESH,
        )

    sent = []
    for k in range(K):
        for d in range(1, E):
            copy = z_copy(d, k, e)
            copy.start()
            sent.append(copy)
        copy = f_copy(0, k)
        copy.start()
        sent.append(copy)

    def forward(k):
        for d in range(1, E):
            z_copy(d, k, (e + E - d) % E).wait_recv()
            copy = f_copy(d, k)
            copy.start()
            sent.append(copy)

    contract = (((1,), (1,)), ((), ()))
    gate_act = up_act = None
    forward(0)
    for k in range(K):
        if k + 1 < K:
            forward(k + 1)
        for d in range(E):
            f_copy(d, k).wait_recv()
        for r in range(2):
            for j in range(E):
                xs[pl.ds((r * E + j) * T, T), pl.ds(k * kw, kw)] = gat[r, j, :, pl.ds(k * kw, kw)]
        rows = xs[:, pl.ds(k * kw, kw)]
        g_copies[k].wait()
        gate_part = lax.dot_general(rows, wg[k], contract, preferred_element_type=jnp.float32)
        u_copies[k].wait()
        up_part = lax.dot_general(rows, wu[k], contract, preferred_element_type=jnp.float32)
        gate_act = gate_part if k == 0 else gate_act + gate_part
        up_act = up_part if k == 0 else up_act + up_part
    hidden = (gate_act / (1.0 + jnp.exp(-gate_act)) * up_act).astype(jnp.bfloat16)

    def d_copy(i, c):
        return pltpu.make_async_remote_copy(
            src_ref=d_out.at[i, c], dst_ref=d_in.at[i, c],
            send_sem=d_send.at[i, c], recv_sem=d_recv.at[i, c],
            device_id=partner, device_id_type=MESH,
        )

    def b_copy(i, c):
        return pltpu.make_async_remote_copy(
            src_ref=b_out.at[i, c], dst_ref=b_in.at[i, c],
            send_sem=b_send.at[i, c], recv_sem=b_recv.at[i, c],
            device_id={"tensor": (x + i) % X}, device_id_type=MESH,
        )

    def c_copy(d, c):
        return pltpu.make_async_remote_copy(
            src_ref=c_out.at[(e + d) % E, c], dst_ref=c_in.at[d, c],
            send_sem=c_send.at[d, c], recv_sem=c_recv.at[d, c],
            device_id={"expert": (e + d) % E}, device_id_type=MESH,
        )

    def down(i, c):
        w_copies[i, c].wait()
        piece = jnp.dot(hidden, wd[i, c], preferred_element_type=jnp.float32)
        d_out[i, c] = piece[half:].astype(jnp.bfloat16)
        copy = d_copy(i, c)
        copy.start()
        sent.append(copy)
        keep[i, c] = piece[:half]

    def over_tensor(i, c):
        d_copy(i, c).wait_recv()
        both = keep[i, c] + d_in[i, c].astype(jnp.float32)
        if i:
            b_out[i, c] = both.astype(jnp.bfloat16)
            copy = b_copy(i, c)
            copy.start()
            sent.append(copy)
        else:
            for d in range(1, X):
                b_copy(d, c).wait_recv()
                both = both + b_in[d, c].astype(jnp.float32)
            both = both.astype(jnp.bfloat16)
            for j in range(E):
                c_out[j, c] = both[j * T:(j + 1) * T]
            for d in range(1, E):
                copy = c_copy(d, c)
                copy.start()
                sent.append(copy)

    down(*order[0])
    for n in range(1, len(order)):
        down(*order[n])
        over_tensor(*order[n - 1])
    over_tensor(*order[-1])

    ids_copy.wait()
    codes_copy.wait()
    weight = codes_v[...].astype(jnp.float32) / 64.0
    shares = []
    for d in range(E):
        expert = ((e + E - d) % E) // 2
        shares.append(jnp.sum(jnp.where(ids_v[...] == expert, weight, 0.0), axis=1, keepdims=True))
    for c in range(C):
        total = shares[0] * c_out[e, c].astype(jnp.float32)
        for d in range(1, E):
            c_copy(d, c).wait_recv()
            total = total + shares[d] * c_in[d, c].astype(jnp.float32)
        out_ref[:, pl.ds(c * cw, cw)] = total.astype(jnp.bfloat16)
    for copy in sent:
        copy.wait_send()


def shards(tokens, expert_ids, gate_codes, w_gate, w_up, w_down):
    T, D = tokens.shape
    E = lax.axis_size("expert")
    X = lax.axis_size("tensor")
    F = w_gate.shape[1]
    K = split_count(D, 4)
    block = D // X
    C = split_count(block, 2)
    kw, cw = D // K, block // C
    half = E * T
    bf16, f32 = jnp.bfloat16, jnp.float32
    dma = pltpu.SemaphoreType.DMA
    hbm = pl.BlockSpec(memory_space=pl.ANY)
    return pl.pallas_call(
        functools.partial(layer, E, X, K, C),
        out_shape=jax.ShapeDtypeStruct((T, block), bf16),
        in_specs=[hbm] * 6,
        out_specs=pl.BlockSpec(memory_space=pltpu.VMEM),
        scratch_shapes=[
            pltpu.VMEM((2, E, T, D), bf16),
            pltpu.VMEM((2 * half, D), bf16),
            pltpu.VMEM(expert_ids.shape, jnp.int32),
            pltpu.VMEM(gate_codes.shape, jnp.int32),
            pltpu.VMEM((K, F, kw), bf16),
            pltpu.VMEM((K, F, kw), bf16),
            pltpu.VMEM((X, C, F, cw), bf16),
            pltpu.VMEM((X, C, half, cw), f32),
            pltpu.VMEM((X, C, half, cw), bf16),
            pltpu.VMEM((X, C, half, cw), bf16),
            pltpu.VMEM((X, C, half, cw), bf16),
            pltpu.VMEM((X, C, half, cw), bf16),
            pltpu.VMEM((E, C, T, cw), bf16),
            pltpu.VMEM((E, C, T, cw), bf16),
            dma((3,)), dma((K,)), dma((K,)), dma((X, C)),
            dma((E, K)), dma((E, K)), dma((E, K)), dma((E, K)),
            dma((X, C)), dma((X, C)), dma((X, C)), dma((X, C)),
            dma((E, C)), dma((E, C)),
        ],
        compiler_params=pltpu.CompilerParams(
            collective_id=0, has_side_effects=True, vmem_limit_bytes=56 * 1024 * 1024
        ),
    )(tokens, expert_ids, gate_codes, w_gate, w_up, w_down)


def solution(mesh):
    return jax.shard_map(
        shards,
        mesh=mesh,
        in_specs=(
            P(("group", "expert", "sub"), None),
            P(("group", "expert", "sub"), None),
            P(("group", "expert", "sub"), None),
            P("expert", ("tensor", "sub"), None),
            P("expert", ("tensor", "sub"), None),
            P("expert", ("tensor", "sub"), None),
        ),
        out_specs=P(("group", "expert", "sub"), "tensor"),
        check_vma=False,
    )
```

time: 52.5 us -> 30.7 us (0.58)
  blocking collectives: 27.1 us -> 0 us
  Pallas kernels: 0 us -> 26.5 us
  matrix products: 10 us -> 0 us
  waiting for transfers between devices: 8.28 us -> 0 us
  starting transfers between devices: 3.38 us -> 0 us
  local copies, waits for them, and re-layouts: 1.83 us -> 4.02 us
  other arithmetic: 1.33 us -> 0 us
    pallas_call x0 -> x1, Pallas kernels: none -> 26.5 us  [shards(): pl.pallas_call(functools.partial(layer, E, X, K, C), out_shape=jax.ShapeD...]
    all_to_all x2 -> x0, blocking collectives: 25 us -> none  [the longest x1 14.3 us: shards(): lax.all_to_all(outgoing.reshape(owners, capacity, features), 'expert', sp...]
    dot_general x4 -> x0, matrix products: 10 us -> none  [the longest x1 5.73 us: shards(): jnp.dot(hidden, w_down[0], preferred_element_type=jnp.float32)]
    all_to_all x1 -> x0, waiting for transfers between devices: 8.28 us -> none  [shards(): lax.all_to_all(run_total, 'expert', split_axis=0, concat_axis=0, tiled=True)]
    all_to_all x1 -> x0, starting transfers between devices: 3.38 us -> none  [shards(): lax.all_to_all(run_total, 'expert', split_axis=0, concat_axis=0, tiled=True)]
    unnamed x5 -> x3, local copies, waits for them, and re-layouts: 0.78 us -> 4.02 us
    all_gather x1 -> x0, blocking collectives: 2.13 us -> none  [shards(): lax.all_gather(arrived, 'sub', axis=1, tiled=True).reshape(-1, features)]
    reduce_sum x4 -> x0, other arithmetic: 1.04 us -> none  [the longest x1 0.89 us: shards(): run_total = jnp.sum(gathered.astype(jnp.float32), axis=2)]
  transfers between devices with their start and end apart: 1 -> 0, of which waited for: 1 -> 0; matrix products, arithmetic and copies ran while one was open for 0% -> 0% of each run, Pallas kernels for 0% -> 0%
where the time goes in v1:
time: 30.7 us; the launch traced here: 30.5 us
  Pallas kernels  26.5 us (86%)
  local copies, waits for them, and re-layouts  4.02 us (13%)
    pallas_call x1, Pallas kernels, shards(): pl.pallas_call(functools.partial(layer, E, X, K, C), out_shape=jax.ShapeD...  26.5 us
    unnamed x3, local copies, waits for them, and re-layouts  4.02 us

profile of v1, /device:TPU:0, one launch (start us, length us, event | category | flops | bytes accessed | tf_op | source)
XLA Modules:
  0.0 30.5 jit_solution(6924404606209300543)
XLA Ops:
  0.0 1.3 %copy.7.ids_hbm = s32[4,2]{1,0:T(4,128)} copy(s32[4,2]{0,1:T(2,128)} %param.7) | data formatting | bytes 64 | tf_op args[1]
  1.3 1.3 %copy.8.codes_hbm = s32[4,2]{1,0:T(4,128)} copy(s32[4,2]{0,1:T(2,128)} %param.8) | data formatting | bytes 64 | tf_op args[2]
  2.7 26.5 %shard_map.64 = bf16[4,3584]{1,0:T(4,128)(2,1)} custom-call(bf16[4,7168]{1,0:T(4,128)(2,1)} %tok_hbm.1, s32[4,2]{1,0:T(4,128)} %copy.7.ids_hbm, s32[4,2]{1,0:T(4,128)} %copy.8.codes_hbm, bf16[1,256,7168]{2,1,0:T(8,128)(2,1)} %wg_hbm.1, bf16[1,256,7168]{2,1,0:T(8,128)(2,1)} %wu_hbm.1, bf16[1,256,7168]{2,1,0:T(8,128)(2,1)} %wd_hbm.1), custom_call_target="tpu_custom_call" | custom-call | tf_op jit(solution)/shard_map/pallas_call | solution.py:210
  29.1 1.4 %copy.10 = bf16[4,3584]{1,0:T(4,128)(2,1)} copy(bf16[4,3584]{1,0:T(4,128)(2,1)} %shard_map.64) | data formatting | bytes 57344

commit v2 on v1

--- a/solution.py
+++ b/solution.py
@@ -171,19 +171,20 @@
                 copy.start()
                 sent.append(copy)
 
-    down(*order[0])
-    for n in range(1, len(order)):
-        down(*order[n])
-        over_tensor(*order[n - 1])
-    over_tensor(*order[-1])
+    for i, c in order:
+        down(i, c)
+    for i, c in order:
+        over_tensor(i, c)
 
     ids_copy.wait()
     codes_copy.wait()
     weight = codes_v[...].astype(jnp.float32) / 64.0
+    diagonal = lax.broadcasted_iota(jnp.int32, (T, T), 0) == lax.broadcasted_iota(jnp.int32, (T, T), 1)
     shares = []
     for d in range(E):
         expert = ((e + E - d) % E) // 2
-        shares.append(jnp.sum(jnp.where(ids_v[...] == expert, weight, 0.0), axis=1, keepdims=True))
+        share = jnp.sum(jnp.where(ids_v[...] == expert, weight, 0.0), axis=0, keepdims=True)
+        shares.append(jnp.sum(jnp.where(diagonal, share, 0.0), axis=1, keepdims=True))
     for c in range(C):
         total = shares[0] * c_out[e, c].astype(jnp.float32)
         for d in range(1, E):
@@ -201,12 +202,12 @@
     F = w_gate.shape[1]
     K = split_count(D, 4)
     block = D // X
-    C = split_count(block, 2)
+    C = split_count(block, 4)
     kw, cw = D // K, block // C
     half = E * T
     bf16, f32 = jnp.bfloat16, jnp.float32
     dma = pltpu.SemaphoreType.DMA
-    hbm = pl.BlockSpec(memory_space=pl.ANY)
+    hbm = pl.BlockSpec(memory_space=pltpu.HBM)
     return pl.pallas_call(
         functools.partial(layer, E, X, K, C),
         out_shape=jax.ShapeDtypeStruct((T, block), bf16),
@@ -215,8 +216,8 @@
         scratch_shapes=[
             pltpu.VMEM((2, E, T, D), bf16),
             pltpu.VMEM((2 * half, D), bf16),
-            pltpu.VMEM(expert_ids.shape, jnp.int32),
-            pltpu.VMEM(gate_codes.shape, jnp.int32),
+            pltpu.VMEM(expert_ids.shape[::-1], jnp.int32),
+            pltpu.VMEM(gate_codes.shape[::-1], jnp.int32),
             pltpu.VMEM((K, F, kw), bf16),
             pltpu.VMEM((K, F, kw), bf16),
             pltpu.VMEM((X, C, F, cw), bf16),
@@ -233,9 +234,9 @@
             dma((E, C)), dma((E, C)),
         ],
         compiler_params=pltpu.CompilerParams(
-            collective_id=0, has_side_effects=True, vmem_limit_bytes=56 * 1024 * 1024
+            collective_id=0, has_side_effects=True, vmem_limit_bytes=67043328 - 44 * 1024
         ),
-    )(tokens, expert_ids, gate_codes, w_gate, w_up, w_down)
+    )(tokens, expert_ids.T, gate_codes.T, w_gate, w_up, w_down)
 
 
 def solution(mesh):

time: 30.7 us -> 28.6 us (0.932)
  local copies, waits for them, and re-layouts: 4.02 us -> 1.37 us
  Pallas kernels: 26.5 us -> 27 us
    unnamed x3 -> x1, local copies, waits for them, and re-layouts: 4.02 us -> 1.37 us
    pallas_call x1, Pallas kernels: 26.5 us -> 27 us  [shards(): pl.pallas_call(functools.partial(layer, E, X, K, C), out_shape=jax.ShapeD...]
where the time goes in v2:
time: 28.6 us; the launch traced here: 28.4 us
  Pallas kernels  27 us (94%)
  local copies, waits for them, and re-layouts  1.37 us (5%)
    pallas_call x1, Pallas kernels, shards(): pl.pallas_call(functools.partial(layer, E, X, K, C), out_shape=jax.ShapeD...  27 us
    unnamed x1, local copies, waits for them, and re-layouts  1.37 us

profile of v2, /device:TPU:0, one launch (start us, length us, event | category | flops | bytes accessed | tf_op | source)
XLA Modules:
  0.0 28.4 jit_solution(15705977611547552593)
XLA Ops:
  0.0 27.0 %shard_map.64 = bf16[4,3584]{1,0:T(4,128)(2,1)} custom-call(bf16[4,7168]{1,0:T(4,128)(2,1)} %tok_hbm.1, s32[2,4]{1,0:T(2,128)} %bitcast.2, s32[2,4]{1,0:T(2,128)} %bitcast.3, bf16[1,256,7168]{2,1,0:T(8,128)(2,1)} %wg_hbm.1, bf16[1,256,7168]{2,1,0:T(8,128)(2,1)} %wu_hbm.1, bf16[1,256,7168]{2,1,0:T(8,128)(2,1)} %wd_hbm.1), custom_call_target="tpu_custom_call" | custom-call | tf_op jit(solution)/shard_map/pallas_call | solution.py:211
  27.0 1.4 %copy.8 = bf16[4,3584]{1,0:T(4,128)(2,1)} copy(bf16[4,3584]{1,0:T(4,128)(2,1)} %shard_map.64) | data formatting | bytes 57344

commit v3 on v2

--- a/solution.py
+++ b/solution.py
@@ -36,19 +36,19 @@
     s = lax.axis_index("sub")
     partner = {"sub": 1 - s}
 
+    barrier = pltpu.get_barrier_semaphore()
+    for d in range(1, E):
+        pl.semaphore_signal(barrier, inc=1, device_id={"expert": (e + d) % E}, device_id_type=MESH)
+    for d in range(1, X):
+        pl.semaphore_signal(barrier, inc=1, device_id={"tensor": (x + d) % X}, device_id_type=MESH)
+    pl.semaphore_signal(barrier, inc=1, device_id=partner, device_id_type=MESH)
+
     tok_copy = pltpu.make_async_copy(tok_hbm, gat.at[0, e], small_sem.at[0])
     tok_copy.start()
     ids_copy = pltpu.make_async_copy(ids_hbm, ids_v, small_sem.at[1])
     codes_copy = pltpu.make_async_copy(codes_hbm, codes_v, small_sem.at[2])
     ids_copy.start()
     codes_copy.start()
-
-    barrier = pltpu.get_barrier_semaphore()
-    for d in range(1, E):
-        pl.semaphore_signal(barrier, inc=1, device_id={"expert": (e + d) % E}, device_id_type=MESH)
-    for d in range(1, X):
-        pl.semaphore_signal(barrier, inc=1, device_id={"tensor": (x + d) % X}, device_id_type=MESH)
-    pl.semaphore_signal(barrier, inc=1, device_id=partner, device_id_type=MESH)
 
     g_copies, u_copies, w_copies = [], [], {}
     for k in range(K):
@@ -202,7 +202,7 @@
     F = w_gate.shape[1]
     K = split_count(D, 4)
     block = D // X
-    C = split_count(block, 4)
+    C = split_count(block, 2)
     kw, cw = D // K, block // C
     half = E * T
     bf16, f32 = jnp.bfloat16, jnp.float32

time: 28.6 us -> 28 us (0.979)
  Pallas kernels: 27 us -> 26.5 us
    pallas_call x1, Pallas kernels: 27 us -> 26.5 us  [shards(): pl.pallas_call(functools.partial(layer, E, X, K, C), out_shape=jax.ShapeD...]
where the time goes in v3:
time: 28 us; the launch traced here: 27.8 us
  Pallas kernels  26.5 us (95%)
  local copies, waits for them, and re-layouts  1.37 us (5%)
    pallas_call x1, Pallas kernels, shards(): pl.pallas_call(functools.partial(layer, E, X, K, C), out_shape=jax.ShapeD...  26.5 us
    unnamed x1, local copies, waits for them, and re-layouts  1.37 us

profile of v3, /device:TPU:0, one launch (start us, length us, event | category | flops | bytes accessed | tf_op | source)
XLA Modules:
  0.0 27.8 jit_solution(13617038258428860478)
XLA Ops:
  0.0 26.5 %shard_map.64 = bf16[4,3584]{1,0:T(4,128)(2,1)} custom-call(bf16[4,7168]{1,0:T(4,128)(2,1)} %tok_hbm.1, s32[2,4]{1,0:T(2,128)} %bitcast.2, s32[2,4]{1,0:T(2,128)} %bitcast.3, bf16[1,256,7168]{2,1,0:T(8,128)(2,1)} %wg_hbm.1, bf16[1,256,7168]{2,1,0:T(8,128)(2,1)} %wu_hbm.1, bf16[1,256,7168]{2,1,0:T(8,128)(2,1)} %wd_hbm.1), custom_call_target="tpu_custom_call" | custom-call | tf_op jit(solution)/shard_map/pallas_call | solution.py:211
  26.5 1.4 %copy.8 = bf16[4,3584]{1,0:T(4,128)(2,1)} copy(bf16[4,3584]{1,0:T(4,128)(2,1)} %shard_map.64) | data formatting | bytes 57344
